TPU v7x, 128 devices: a whole 4x4x4 slice. The times are simulated.
128 devices in a mesh: dp: 8 (over x, core), rollout: 16 (over y, z).
Axes of the slice: x: 4, y: 4, z: 4, core: 2. Of those that a mesh axis runs over, the one named last changes fastest.
Arguments:
- queries: bfloat16 [128, 512, 2560], P(('dp', 'rollout')), may hold values from -100 to 100
- resp_keys: bfloat16 [128, 512, 512], P(('dp', 'rollout')), may hold values from -5 to 5
- resp_values: bfloat16 [128, 512, 512], P(('dp', 'rollout')), may hold values from -6 to 6
- prompt_keys: bfloat16 [8, 256, 512], P('dp', 'rollout'), may hold values from -6 to 6
- prompt_values: bfloat16 [8, 256, 512], P('dp', 'rollout'), may hold values from -6 to 6
- d_out: bfloat16 [128, 512, 2560], P(('dp', 'rollout')), may hold values from -6 to 6
- lengths: int32 [128], replicated, may hold values from 64 to 512
- owner: int32 [128], replicated, may hold values from 0 to 7
Outputs:
- attn_out: bfloat16 [128, 512, 2560], P(('dp', 'rollout'))
- d_queries: bfloat16 [128, 512, 2560], P(('dp', 'rollout'))
- d_resp_keys: bfloat16 [128, 512, 512], P(('dp', 'rollout'))
- d_resp_values: bfloat16 [128, 512, 512], P(('dp', 'rollout'))
- d_prompt_keys: float32 [8, 256, 512], P('dp', 'rollout')
- d_prompt_values: float32 [8, 256, 512], P('dp', 'rollout')
Inputs may be any that keep to these rules, and one draw needn't show every extreme that they name: `lengths`: rows of a block at or past its length are padding.
All inputs are finite; a program needn't handle non-finite values.
Results may differ from a plain program's by a relative error of at most 0.0071.
Values may be sent and summed in bfloat16 or wider, within the bound.
No kernel may reach another device: no remote copies, remote signals or barrier semaphores. Data moves between devices by JAX's collectives and lax.ppermute only.
A program may use at most 128 MiB of HBM per device.

v0:
```python
import jax
import jax.numpy as jnp
from jax import lax
from jax.sharding import PartitionSpec as P

HEAD_DIM = 128
BLOCK = 512
TILE = 128


def cut_along(shard, dim, count):
    dims = shard.shape
    pieces = shard.reshape(*dims[:dim], count, dims[dim] // count, *dims[dim + 1 :])
    return jnp.moveaxis(pieces, dim, 0)


def sent_and_summed(shard, axis, dim):
    pieces = cut_along(shard, dim, lax.axis_size(axis))
    arrived = lax.all_to_all(pieces, axis, split_axis=0, concat_axis=0, tiled=True)
    return arrived.astype(jnp.float32).sum(axis=0)


def attend(q_rows, d_rows, offset, stride, length, keys, values):
    rows = q_rows.shape[0]
    span = keys.shape[0]
    kv_heads = keys.shape[1] // HEAD_DIM
    group = q_rows.shape[1] // keys.shape[1]
    key_heads = keys.reshape(span, kv_heads, HEAD_DIM)
    val_heads = values.reshape(span, kv_heads, HEAD_DIM)
    key_pos = jnp.arange(span, dtype=jnp.int32) - (span - BLOCK)
    live_rows = jnp.clip((length - offset + stride - 1) // stride, 0, rows)
    turns = (live_rows + TILE - 1) // TILE
    scale = HEAD_DIM ** (-0.5)

    def step(turn, carry):
        out_all, dq_all, dk_sum, dv_sum = carry
        start = (turn * TILE).astype(jnp.int32)
        qt = lax.dynamic_slice_in_dim(q_rows, start, TILE, 0).reshape(
            TILE, kv_heads, group, HEAD_DIM
        )
        dt = lax.dynamic_slice_in_dim(d_rows, start, TILE, 0)
        pos = offset + stride * (start + jnp.arange(TILE, dtype=jnp.int32))
        live = pos < length
        dt = jnp.where(live[:, None], dt, jnp.zeros_like(dt)).reshape(
            TILE, kv_heads, group, HEAD_DIM
        )
        scores = (
            jnp.einsum("tkgd,skd->kgts", qt, key_heads, preferred_element_type=jnp.float32) * scale
        )
        allowed = key_pos[None, :] <= pos[:, None]
        scores = jnp.where(allowed, scores, -1e30)
        top = jnp.max(scores, axis=-1, keepdims=True)
        expd = jnp.exp(scores - top)
        probs = expd / jnp.sum(expd, axis=-1, keepdims=True)
        weights = probs.astype(jnp.bfloat16)
        out = jnp.einsum("kgts,skd->tkgd", weights, val_heads, preferred_element_type=jnp.float32)
        out = out * live.astype(jnp.float32)[:, None, None, None]
        dprob = jnp.einsum("tkgd,skd->kgts", dt, val_heads, preferred_element_type=jnp.float32)
        delta = jnp.einsum("tkgd,tkgd->kgt", dt.astype(jnp.float32), out)
        dscore = (probs * (dprob - delta[..., None]) * scale).astype(jnp.bfloat16)
        dq = jnp.einsum("kgts,skd->tkgd", dscore, key_heads, preferred_element_type=jnp.float32)
        dk_sum = dk_sum + jnp.einsum(
            "kgts,tkgd->skd", dscore, qt, preferred_element_type=jnp.float32
        )
        dv_sum = dv_sum + jnp.einsum(
            "kgts,tkgd->skd", weights, dt, preferred_element_type=jnp.float32
        )
        out_all = lax.dynamic_update_slice_in_dim(
            out_all, out.reshape(TILE, -1).astype(jnp.bfloat16), start, 0
        )
        dq_all = lax.dynamic_update_slice_in_dim(
            dq_all, dq.reshape(TILE, -1).astype(jnp.bfloat16), start, 0
        )
        return (out_all, dq_all, dk_sum, dv_sum)

    init = (
        jnp.zeros((rows, q_rows.shape[1]), jnp.bfloat16),
        jnp.zeros((rows, q_rows.shape[1]), jnp.bfloat16),
        jnp.zeros((span, kv_heads, HEAD_DIM), jnp.float32),
        jnp.zeros((span, kv_heads, HEAD_DIM), jnp.float32),
    )
    out_all, dq_all, dk_sum, dv_sum = lax.fori_loop(jnp.int32(0), turns, step, init)
    return (out_all, dq_all, dk_sum.reshape(span, -1), dv_sum.reshape(span, -1))


def block_inputs(whole_prompt, group_index, keys_block, values_block, width_k):
    prompt_pair = lax.dynamic_index_in_dim(whole_prompt, group_index, 0, keepdims=False)
    keys = jnp.concatenate([prompt_pair[:, :width_k], keys_block], axis=0)
    values = jnp.concatenate([prompt_pair[:, width_k:], values_block], axis=0)
    return (keys, values)


def per_device(queries, resp_keys, resp_values, prompt_keys, prompt_values, d_out, lengths, owner):
    rollout_count = lax.axis_size("rollout")
    groups = lax.axis_size("dp")
    row_base = lax.axis_index("dp") * rollout_count
    here = row_base + lax.axis_index("rollout")
    shard_rows = prompt_keys.shape[1]
    prompt_n = shard_rows * rollout_count
    width_k = prompt_keys.shape[2]
    local_pair = jnp.concatenate([prompt_keys[0], prompt_values[0]], axis=1)
    gathered = lax.all_gather(local_pair, ("dp", "rollout"), axis=0, tiled=True)
    whole_prompt = gathered.reshape(groups, prompt_n, 2 * width_k)
    group_ids = jnp.arange(groups, dtype=jnp.int32)
    own_group = owner[here]
    own_keys, own_values = block_inputs(
        whole_prompt, own_group, resp_keys[0], resp_values[0], width_k
    )
    row_owner = lax.dynamic_slice_in_dim(owner, row_base, rollout_count, 0)
    out, dq, dk_all, dv_all = attend(
        queries[0], d_out[0], 0, 1, lengths[here], own_keys, own_values
    )
    dk_resp = dk_all[prompt_n:]
    dv_resp = dv_all[prompt_n:]
    terms = jnp.concatenate([dk_all[:prompt_n], dv_all[:prompt_n]], axis=1)[None]
    source_groups = row_owner[None]
    pieces = terms.reshape(terms.shape[0], rollout_count, shard_rows, 2 * width_k)
    received = lax.all_to_all(
        pieces.astype(jnp.bfloat16), "rollout", split_axis=1, concat_axis=1, tiled=True
    ).astype(pieces.dtype)
    picks = (source_groups[:, :, None] == group_ids[None, None, :]).astype(jnp.float32)
    by_group = jnp.einsum("msg,msrc->grc", picks, received, precision=lax.Precision.HIGHEST)
    summed = sent_and_summed(by_group.astype(jnp.bfloat16), "dp", 0)[0]
    return (
        out[None],
        dq[None],
        dk_resp.astype(jnp.bfloat16)[None],
        dv_resp.astype(jnp.bfloat16)[None],
        summed[None, :, :width_k],
        summed[None, :, width_k:],
    )


def solution(mesh):
    placed = (
        P(("dp", "rollout"), None, None),
        P(("dp", "rollout"), None, None),
        P(("dp", "rollout"), None, None),
        P("dp", "rollout", None),
        P("dp", "rollout", None),
        P(("dp", "rollout"), None, None),
        P(),
        P(),
    )
    return jax.shard_map(
        per_device,
        mesh=mesh,
        in_specs=placed,
        out_specs=(
            P(("dp", "rollout"), None, None),
            P(("dp", "rollout"), None, None),
            P(("dp", "rollout"), None, None),
            P(("dp", "rollout"), None, None),
            P("dp", "rollout", None),
            P("dp", "rollout", None),
        ),
        check_vma=False,
    )
```

profile of v0, /device:TPU:1, one launch (start us, length us, event | category | flops | bytes accessed | tf_op | source)
XLA Modules:
  0.0 223.8 jit_solution(10658430492384995604)
XLA Ops:
  7.2 1.4 pad_maximum_fusion.2
  14.3 2.0 copy.50
  16.4 4.5 %copy.47 = bf16[1,512,2560]{1,2,0:T(8,128)(2,1)} copy(bf16[1,512,2560]{2,1,0:T(8,128)(2,1)} %param.10) | data formatting | bytes 5242880 | tf_op args[0]
  20.9 2.6 %copy.51 = bf16[1,512,2560]{1,2,0:T(8,128)(2,1)} copy(bf16[1,512,2560]{2,1,0:T(8,128)(2,1)S(1)} %copy-done.5) | data formatting | bytes 5242880 | tf_op args[5]
  24.3 57.5 %all-gather.2.cloned.1.call-done = bf16[2048,1024]{1,0:T(8,128)(2,1)} async-done(((bf16[16,1024]{1,0:T(8,128)(2,1)}), bf16[2048,1024]{1,0:T(8,128)(2,1)}) %all-gather.2.cloned.1.call-update) | async-done | bytes 4194320 | tf_op jit(solution)/shard_map/all_gather | solution.py:102
  86.8 1.7 broadcast.73.clone2
  88.4 1.7 broadcast.73.clone
  90.1 95.3 %while.17 = (s32[]{:T(128)}, bf16[512,2560]{1,0:T(8,128)(2,1)}, bf16[512,2560]{1,0:T(8,128)(2,1)}, f32[768,4,128]{0,2,1:T(8,128)}, f32[768,4,128]{0,2,1:T(8,128)...) while((s32[]{:T(128)}, bf16[512,2560]{1,0:T(8,128)(2,1)}, ...), condition=%wide.region_3.4_spmd.clone, body=%wide.region_0.3_spmd.clone.sunk | while | flops 3048635904 | bytes 116517448 | solution.py:82
  90.9 1.5 dynamic-slice_select_fusion.2
  92.3 2.4 %fusion.68 = f32[4,128,5,768]{3,1,2,0:T(8,128)S(1)} fusion(bf16[128,4,5,128]{0,3,2,1:T(8,128)(2,1)S(1)} %bitcast.145, bf16[768,4,128]{0,2,1:T(8,128)(2,1)} %get-tuple-element.278), kind=kOutput, calls=%fused_computation.26.clone.1 | convolution fusion | flops 503316480 | bytes 9306112 | tf_op jit(solution)/shard_map/while/body/tkgd,skd->kgts/dot_general | solution.py:48
  94.7 3.7 %fusion.69 = (f32[4,5,128]{2,1,0:T(8,128)S(1)}, f32[4,5,128,768]{3,2,1,0:T(8,128)S(1)}) fusion(f32[4,128,5,768]{3,1,2,0:T(8,128)S(1)} %fusion.68, pred[128,768]{1,0:T(8,128)(4,1)S(1)} %broadcast_compare_fusion.4), kind=kOutput, calls=%fused_computation.54.clone.1 | output fusion | flops 11797247 | bytes 15837184 | tf_op jit(solution)/shard_map/while/body/sub | solution.py:53
  101.8 3.6 %fusion.72 = bf16[4,5,128,768]{3,2,1,0:T(8,128)(2,1)} fusion(f32[4,5,128]{2,1,0:T(8,128)S(1)} %get-tuple-element.240, f32[4,5,128,768]{3,2,1,0:T(8,128)S(1)} %get-tuple-element.237, f32[4,5,128]{2,1,0:T(8,128)S(1)} %get-tuple-element.238, bf16[128,4,5,128]{0,3,2,1:T(8,128)(2,1)S(1)} %bitcast.149, bf16[768,4,128]{2,0,1:T(8,128)(2,1)S(1)} %copy-done.7), kind=kOutput, calls=%fused_computation.5.clone.1 | convolution fusion | flops 513146880 | bytes 13258752 | tf_op jit(solution)/shard_map/while/body/tkgd,skd->kgts/dot_general | solution.py:58
  105.7 3.7 %convolution_convert_fusion.3 = bf16[4,5,128,128]{2,3,1,0:T(8,128)(2,1)S(1)} fusion(bf16[4,5,128,768]{3,2,1,0:T(8,128)(2,1)} %fusion.72, bf16[768,4,128]{0,2,1:T(8,128)(2,1)} %get-tuple-element.278), kind=kOutput, calls=%fused_computation.19.clone.1 | convolution fusion | flops 503644160 | bytes 5373952 | tf_op jit(solution)/shard_map/while/body/kgts,skd->tkgd/dot_general | solution.py:61
  114.7 1.5 dynamic-slice_select_fusion.2
  116.2 2.4 %fusion.68 = f32[4,128,5,768]{3,1,2,0:T(8,128)S(1)} fusion(bf16[128,4,5,128]{0,3,2,1:T(8,128)(2,1)S(1)} %bitcast.145, bf16[768,4,128]{0,2,1:T(8,128)(2,1)} %get-tuple-element.278), kind=kOutput, calls=%fused_computation.26.clone.1 | convolution fusion | flops 503316480 | bytes 9306112 | tf_op jit(solution)/shard_map/while/body/tkgd,skd->kgts/dot_general | solution.py:48
  118.5 3.7 %fusion.69 = (f32[4,5,128]{2,1,0:T(8,128)S(1)}, f32[4,5,128,768]{3,2,1,0:T(8,128)S(1)}) fusion(f32[4,128,5,768]{3,1,2,0:T(8,128)S(1)} %fusion.68, pred[128,768]{1,0:T(8,128)(4,1)S(1)} %broadcast_compare_fusion.4), kind=kOutput, calls=%fused_computation.54.clone.1 | output fusion | flops 11797247 | bytes 15837184 | tf_op jit(solution)/shard_map/while/body/sub | solution.py:53
  125.7 3.6 %fusion.72 = bf16[4,5,128,768]{3,2,1,0:T(8,128)(2,1)} fusion(f32[4,5,128]{2,1,0:T(8,128)S(1)} %get-tuple-element.240, f32[4,5,128,768]{3,2,1,0:T(8,128)S(1)} %get-tuple-element.237, f32[4,5,128]{2,1,0:T(8,128)S(1)} %get-tuple-element.238, bf16[128,4,5,128]{0,3,2,1:T(8,128)(2,1)S(1)} %bitcast.149, bf16[768,4,128]{2,0,1:T(8,128)(2,1)S(1)} %copy-done.7), kind=kOutput, calls=%fused_computation.5.clone.1 | convolution fusion | flops 513146880 | bytes 13258752 | tf_op jit(solution)/shard_map/while/body/tkgd,skd->kgts/dot_general | solution.py:58
  129.6 3.7 %convolution_convert_fusion.3 = bf16[4,5,128,128]{2,3,1,0:T(8,128)(2,1)S(1)} fusion(bf16[4,5,128,768]{3,2,1,0:T(8,128)(2,1)} %fusion.72, bf16[768,4,128]{0,2,1:T(8,128)(2,1)} %get-tuple-element.278), kind=kOutput, calls=%fused_computation.19.clone.1 | convolution fusion | flops 503644160 | bytes 5373952 | tf_op jit(solution)/shard_map/while/body/kgts,skd->tkgd/dot_general | solution.py:61
  138.5 1.5 dynamic-slice_select_fusion.2
  140.0 2.4 %fusion.68 = f32[4,128,5,768]{3,1,2,0:T(8,128)S(1)} fusion(bf16[128,4,5,128]{0,3,2,1:T(8,128)(2,1)S(1)} %bitcast.145, bf16[768,4,128]{0,2,1:T(8,128)(2,1)} %get-tuple-element.278), kind=kOutput, calls=%fused_computation.26.clone.1 | convolution fusion | flops 503316480 | bytes 9306112 | tf_op jit(solution)/shard_map/while/body/tkgd,skd->kgts/dot_general | solution.py:48
  142.4 3.7 %fusion.69 = (f32[4,5,128]{2,1,0:T(8,128)S(1)}, f32[4,5,128,768]{3,2,1,0:T(8,128)S(1)}) fusion(f32[4,128,5,768]{3,1,2,0:T(8,128)S(1)} %fusion.68, pred[128,768]{1,0:T(8,128)(4,1)S(1)} %broadcast_compare_fusion.4), kind=kOutput, calls=%fused_computation.54.clone.1 | output fusion | flops 11797247 | bytes 15837184 | tf_op jit(solution)/shard_map/while/body/sub | solution.py:53
  149.5 3.6 %fusion.72 = bf16[4,5,128,768]{3,2,1,0:T(8,128)(2,1)} fusion(f32[4,5,128]{2,1,0:T(8,128)S(1)} %get-tuple-element.240, f32[4,5,128,768]{3,2,1,0:T(8,128)S(1)} %get-tuple-element.237, f32[4,5,128]{2,1,0:T(8,128)S(1)} %get-tuple-element.238, bf16[128,4,5,128]{0,3,2,1:T(8,128)(2,1)S(1)} %bitcast.149, bf16[768,4,128]{2,0,1:T(8,128)(2,1)S(1)} %copy-done.7), kind=kOutput, calls=%fused_computation.5.clone.1 | convolution fusion | flops 513146880 | bytes 13258752 | tf_op jit(solution)/shard_map/while/body/tkgd,skd->kgts/dot_general | solution.py:58
  153.4 3.7 %convolution_convert_fusion.3 = bf16[4,5,128,128]{2,3,1,0:T(8,128)(2,1)S(1)} fusion(bf16[4,5,128,768]{3,2,1,0:T(8,128)(2,1)} %fusion.72, bf16[768,4,128]{0,2,1:T(8,128)(2,1)} %get-tuple-element.278), kind=kOutput, calls=%fused_computation.19.clone.1 | convolution fusion | flops 503644160 | bytes 5373952 | tf_op jit(solution)/shard_map/while/body/kgts,skd->tkgd/dot_general | solution.py:61
  162.4 1.5 dynamic-slice_select_fusion.2
  163.8 2.4 %fusion.68 = f32[4,128,5,768]{3,1,2,0:T(8,128)S(1)} fusion(bf16[128,4,5,128]{0,3,2,1:T(8,128)(2,1)S(1)} %bitcast.145, bf16[768,4,128]{0,2,1:T(8,128)(2,1)} %get-tuple-element.278), kind=kOutput, calls=%fused_computation.26.clone.1 | convolution fusion | flops 503316480 | bytes 9306112 | tf_op jit(solution)/shard_map/while/body/tkgd,skd->kgts/dot_general | solution.py:48
  166.2 3.7 %fusion.69 = (f32[4,5,128]{2,1,0:T(8,128)S(1)}, f32[4,5,128,768]{3,2,1,0:T(8,128)S(1)}) fusion(f32[4,128,5,768]{3,1,2,0:T(8,128)S(1)} %fusion.68, pred[128,768]{1,0:T(8,128)(4,1)S(1)} %broadcast_compare_fusion.4), kind=kOutput, calls=%fused_computation.54.clone.1 | output fusion | flops 11797247 | bytes 15837184 | tf_op jit(solution)/shard_map/while/body/sub | solution.py:53
  173.3 3.6 %fusion.72 = bf16[4,5,128,768]{3,2,1,0:T(8,128)(2,1)} fusion(f32[4,5,128]{2,1,0:T(8,128)S(1)} %get-tuple-element.240, f32[4,5,128,768]{3,2,1,0:T(8,128)S(1)} %get-tuple-element.237, f32[4,5,128]{2,1,0:T(8,128)S(1)} %get-tuple-element.238, bf16[128,4,5,128]{0,3,2,1:T(8,128)(2,1)S(1)} %bitcast.149, bf16[768,4,128]{2,0,1:T(8,128)(2,1)S(1)} %copy-done.7), kind=kOutput, calls=%fused_computation.5.clone.1 | convolution fusion | flops 513146880 | bytes 13258752 | tf_op jit(solution)/shard_map/while/body/tkgd,skd->kgts/dot_general | solution.py:58
  177.2 3.7 %convolution_convert_fusion.3 = bf16[4,5,128,128]{2,3,1,0:T(8,128)(2,1)S(1)} fusion(bf16[4,5,128,768]{3,2,1,0:T(8,128)(2,1)} %fusion.72, bf16[768,4,128]{0,2,1:T(8,128)(2,1)} %get-tuple-element.278), kind=kOutput, calls=%fused_computation.19.clone.1 | convolution fusion | flops 503644160 | bytes 5373952 | tf_op jit(solution)/shard_map/while/body/kgts,skd->tkgd/dot_general | solution.py:61
  188.4 4.4 %all-to-all-start = ((bf16[1,16,16,1024]{3,2,0,1:T(8,128)(2,1)}), bf16[1,16,16,1024]{3,2,0,1:T(8,128)(2,1)S(1)}, u32[]{:S(2)}, u32[]{:S(2)}) async-start(bf16[1,16,16,1024]{3,2,0,1:T(8,128)(2,1)} %maximum_bitcast_fusion), calls=%async_computation | async-start | bytes 1048576 | tf_op jit(solution)/shard_map/all_to_all | solution.py:118
  192.8 10.0 %all-to-all-done = bf16[1,16,16,1024]{3,2,0,1:T(8,128)(2,1)S(1)} async-done(((bf16[1,16,16,1024]{3,2,0,1:T(8,128)(2,1)}), bf16[1,16,16,1024]{3,2,0,1:T(8,128)(2,1)S(1)}, u32[]{:S(2)}, u32[]{:S(2)}) %all-to-all-start) | async-done | bytes 524320 | tf_op jit(solution)/shard_map/all_to_all | solution.py:118
  204.1 5.6 %all-to-all-start.1 = ((bf16[8,1,16,1024]{3,2,1,0:T(8,128)(2,1)}), bf16[8,1,16,1024]{3,2,1,0:T(8,128)(2,1)S(1)}, u32[]{:S(2)}, u32[]{:S(2)}) async-start(bf16[8,1,16,1024]{3,2,1,0:T(8,128)(2,1)} %copy.61), calls=%async_computation.1 | async-start | bytes 524288 | tf_op jit(solution)/shard_map/all_to_all | solution.py:19
  211.8 4.4 %all-to-all-done.1 = bf16[8,1,16,1024]{3,2,1,0:T(8,128)(2,1)S(1)} async-done(((bf16[8,1,16,1024]{3,2,1,0:T(8,128)(2,1)}), bf16[8,1,16,1024]{3,2,1,0:T(8,128)(2,1)S(1)}, u32[]{:S(2)}, u32[]{:S(2)}) %all-to-all-start.1) | async-done | bytes 262176 | tf_op jit(solution)/shard_map/all_to_all | solution.py:19
  (122 shorter events, 51.1 us)
Async XLA Ops:
  7.2 74.6 %all-gather.2.cloned.1.call-start = ((), (), s32[]{:S(2)}) async-start(), calls=%async_computation.2 | async-start | bytes 4227072 | tf_op jit(solution)/shard_map/all_gather | solution.py:102
  16.4 4.6 %copy-start.5 = (bf16[1,512,2560]{2,1,0:T(8,128)(2,1)S(1)}, bf16[1,512,2560]{2,1,0:T(8,128)(2,1)}, u32[]{:S(2)}) copy-start(bf16[1,512,2560]{2,1,0:T(8,128)(2,1)} %param.15) | copy-start | bytes 7864324
  23.5 59.6 %copy-start.6 = (bf16[1,512,512]{1,2,0:T(8,128)(2,1)S(1)}, bf16[1,512,512]{1,2,0:T(8,128)(2,1)}, u32[]{:S(2)}) copy-start(bf16[1,512,512]{1,2,0:T(8,128)(2,1)} %copy.50) | copy-start | bytes 1572868
  98.4 1.1 copy-start.7
  105.7 3.8 %copy-start = (bf16[4,5,128,768]{3,2,1,0:T(8,128)(2,1)S(1)}, bf16[4,5,128,768]{3,2,1,0:T(8,128)(2,1)}, u32[]{:S(2)}) copy-start(bf16[4,5,128,768]{3,2,1,0:T(8,128)(2,1)} %fusion.72) | copy-start | bytes 11796484 | tf_op jit(solution)/shard_map/while
  105.7 4.0 %copy-start.1 = (f32[768,4,128]{0,2,1:T(8,128)S(1)}, f32[768,4,128]{0,2,1:T(8,128)}, u32[]{:S(2)}) copy-start(f32[768,4,128]{0,2,1:T(8,128)} %get-tuple-element.259) | copy-start | bytes 4718596 | tf_op jit(solution)/shard_map/while
  110.7 1.2 copy-start.2
  122.2 1.1 copy-start.7
  129.6 3.8 %copy-start = (bf16[4,5,128,768]{3,2,1,0:T(8,128)(2,1)S(1)}, bf16[4,5,128,768]{3,2,1,0:T(8,128)(2,1)}, u32[]{:S(2)}) copy-start(bf16[4,5,128,768]{3,2,1,0:T(8,128)(2,1)} %fusion.72) | copy-start | bytes 11796484 | tf_op jit(solution)/shard_map/while
  129.6 4.0 %copy-start.1 = (f32[768,4,128]{0,2,1:T(8,128)S(1)}, f32[768,4,128]{0,2,1:T(8,128)}, u32[]{:S(2)}) copy-start(f32[768,4,128]{0,2,1:T(8,128)} %get-tuple-element.259) | copy-start | bytes 4718596 | tf_op jit(solution)/shard_map/while
  134.6 1.2 copy-start.2
  146.1 1.1 copy-start.7
  153.4 3.8 %copy-start = (bf16[4,5,128,768]{3,2,1,0:T(8,128)(2,1)S(1)}, bf16[4,5,128,768]{3,2,1,0:T(8,128)(2,1)}, u32[]{:S(2)}) copy-start(bf16[4,5,128,768]{3,2,1,0:T(8,128)(2,1)} %fusion.72) | copy-start | bytes 11796484 | tf_op jit(solution)/shard_map/while
  153.4 4.0 %copy-start.1 = (f32[768,4,128]{0,2,1:T(8,128)S(1)}, f32[768,4,128]{0,2,1:T(8,128)}, u32[]{:S(2)}) copy-start(f32[768,4,128]{0,2,1:T(8,128)} %get-tuple-element.259) | copy-start | bytes 4718596 | tf_op jit(solution)/shard_map/while
  158.4 1.2 copy-start.2
  169.9 1.1 copy-start.7
  177.2 3.8 %copy-start = (bf16[4,5,128,768]{3,2,1,0:T(8,128)(2,1)S(1)}, bf16[4,5,128,768]{3,2,1,0:T(8,128)(2,1)}, u32[]{:S(2)}) copy-start(bf16[4,5,128,768]{3,2,1,0:T(8,128)(2,1)} %fusion.72) | copy-start | bytes 11796484 | tf_op jit(solution)/shard_map/while
  177.2 4.0 %copy-start.1 = (f32[768,4,128]{0,2,1:T(8,128)S(1)}, f32[768,4,128]{0,2,1:T(8,128)}, u32[]{:S(2)}) copy-start(f32[768,4,128]{0,2,1:T(8,128)} %get-tuple-element.259) | copy-start | bytes 4718596 | tf_op jit(solution)/shard_map/while
  182.2 1.2 copy-start.2
  185.4 1.7 copy-start.3
  185.5 0.9 copy-start.4
  187.1 5.6 %copy-start.8 = (s32[128]{0:T(128)S(1)}, s32[128]{0:T(128)}, u32[]{:S(2)}) copy-start(s32[128]{0:T(128)} %param.17) | copy-start | bytes 1540
  188.4 21.4 %slice-start = ((bf16[768,4,128]{0,2,1:T(8,128)(2,1)}), bf16[512,4,128]{0,2,1:T(8,128)(2,1)S(1)}, s32[]{:S(2)}) async-start(bf16[768,4,128]{0,2,1:T(8,128)(2,1)} %copy-done.4), calls=%async_computation.3 | async-start | bytes 1048576 | tf_op jit(solution)/shard_map/slice | solution.py:114
  188.4 14.5 %all-to-all-start = ((bf16[1,16,16,1024]{3,2,0,1:T(8,128)(2,1)}), bf16[1,16,16,1024]{3,2,0,1:T(8,128)(2,1)S(1)}, u32[]{:S(2)}, u32[]{:S(2)}) async-start(bf16[1,16,16,1024]{3,2,0,1:T(8,128)(2,1)} %maximum_bitcast_fusion), calls=%async_computation | async-start | bytes 1048576 | tf_op jit(solution)/shard_map/all_to_all | solution.py:118
  204.1 12.1 %all-to-all-start.1 = ((bf16[8,1,16,1024]{3,2,1,0:T(8,128)(2,1)}), bf16[8,1,16,1024]{3,2,1,0:T(8,128)(2,1)S(1)}, u32[]{:S(2)}, u32[]{:S(2)}) async-start(bf16[8,1,16,1024]{3,2,1,0:T(8,128)(2,1)} %copy.61), calls=%async_computation.1 | async-start | bytes 524288 | tf_op jit(solution)/shard_map/all_to_all | solution.py:19
Sparse Core Ops, SparseCore 0:
  11.7 70.0 all-gather.1
where the time goes:
time: 225 us; the launch traced here: 224 us
  waiting for transfers between devices  72 us (32%)
  matrix products  52.5 us (23%)
  local copies, waits for them, and re-layouts  42.1 us (19%)
  other arithmetic  29.7 us (13%)
  between operations  16.9 us (8%)
  starting transfers between devices  10 us (4%)
    all_gather x1, waiting for transfers between devices, per_device(): gathered = lax.all_gather(local_pair, ('dp', 'rollout'), axis=0, tiled=True)  57.5 us
    dot_general x4, matrix products, step(): jnp.einsum('kgts,skd->tkgd', dscore, key_heads, preferred_element_type=jn...  14.9 us
    sub x4, other arithmetic, step(): expd = jnp.exp(scores - top)  14.7 us
    dot_general x4, matrix products, step(): jnp.einsum('tkgd,skd->kgts', dt, val_heads, preferred_element_type=jnp.fl...  14.5 us
    unnamed x16, local copies, waits for them, and re-layouts  13.2 us
    all_to_all x1, waiting for transfers between devices, per_device(): lax.all_to_all(pieces.astype(jnp.bfloat16), 'rollout', split_axis=1, conc...  10 us
    dot_general x4, matrix products, step(): jnp.einsum('tkgd,skd->kgts', qt, key_heads, preferred_element_type=jnp.fl...  9.42 us
    while x32, local copies, waits for them, and re-layouts  7.41 us
  transfers between devices with their start and end apart: 3, of which 3 were waited for; matrix products, arithmetic and copies ran while one was open for 7% of the time, Pallas kernels for 0%

commit v1 on v0

--- a/solution.py
+++ b/solution.py
@@ -99,7 +99,12 @@
     prompt_n = shard_rows * rollout_count
     width_k = prompt_keys.shape[2]
     local_pair = jnp.concatenate([prompt_keys[0], prompt_values[0]], axis=1)
-    gathered = lax.all_gather(local_pair, ("dp", "rollout"), axis=0, tiled=True)
+    gathered = jnp.concatenate(
+        lax.all_to_all(
+            jnp.stack([local_pair] * lax.axis_size(("dp", "rollout"))), ("dp", "rollout"), 0, 0
+        ),
+        axis=0,
+    )
     whole_prompt = gathered.reshape(groups, prompt_n, 2 * width_k)
     group_ids = jnp.arange(groups, dtype=jnp.int32)
     own_group = owner[here]

time: 225 us -> 204 us (0.907)
  waiting for transfers between devices: 72 us -> 52.1 us
  between operations: 16.9 us -> 3.53 us
  starting transfers between devices: 10 us -> 22 us
    all_gather x1 -> x0, waiting for transfers between devices: 57.5 us -> none  [per_device(): gathered = lax.all_gather(local_pair, ('dp', 'rollout'), axis=0, tiled=True)]
    all_to_all x0 -> x1, waiting for transfers between devices: none -> 37.6 us  [per_device(): lax.all_to_all(jnp.stack([local_pair] * lax.axis_size(('dp', 'rollout')))...]
    all_to_all x0 -> x1, starting transfers between devices: none -> 11.9 us  [per_device(): lax.all_to_all(jnp.stack([local_pair] * lax.axis_size(('dp', 'rollout')))...]
    another operation x4 -> x5, local copies, waits for them, and re-layouts: 4.74 us -> 7.24 us
    unnamed x16 -> x19, local copies, waits for them, and re-layouts: 13.2 us -> 12.9 us
where the time goes in v1:
time: 204 us; the launch traced here: 203 us
  matrix products  52.4 us (26%)
  waiting for transfers between devices  52.1 us (26%)
  local copies, waits for them, and re-layouts  43.3 us (21%)
  other arithmetic  29.1 us (14%)
  starting transfers between devices  22 us (11%)
  between operations  3.53 us (2%)
    all_to_all x1, waiting for transfers between devices, per_device(): lax.all_to_all(jnp.stack([local_pair] * lax.axis_size(('dp', 'rollout')))...  37.6 us
    dot_general x4, matrix products, step(): jnp.einsum('kgts,skd->tkgd', dscore, key_heads, preferred_element_type=jn...  15 us
    sub x4, other arithmetic, step(): expd = jnp.exp(scores - top)  14.7 us
    dot_general x4, matrix products, step(): jnp.einsum('tkgd,skd->kgts', dt, val_heads, preferred_element_type=jnp.fl...  14.5 us
    unnamed x19, local copies, waits for them, and re-layouts  12.9 us
    all_to_all x1, starting transfers between devices, per_device(): lax.all_to_all(jnp.stack([local_pair] * lax.axis_size(('dp', 'rollout')))...  11.9 us
    all_to_all x1, waiting for transfers between devices, per_device(): lax.all_to_all(pieces.astype(jnp.bfloat16), 'rollout', split_axis=1, conc...  10.1 us
    dot_general x4, matrix products, step(): jnp.einsum('tkgd,skd->kgts', qt, key_heads, preferred_element_type=jnp.fl...  9.41 us
  transfers between devices with their start and end apart: 3, of which 3 were waited for; matrix products, arithmetic and copies ran while one was open for 7% of the time, Pallas kernels for 0%

profile of v1, /device:TPU:1, one launch (start us, length us, event | category | flops | bytes accessed | tf_op | source)
XLA Modules:
  0.0 203.0 jit_solution(6642180245812611647)
XLA Ops:
  1.4 2.5 %stack.2 = bf16[128,16,1024]{2,1,0:T(8,128)(2,1)} broadcast(bf16[16,1024]{1,0:T(8,128)(2,1)S(1)} %pad_maximum_fusion.2), dimensions={1,2} | broadcast | bytes 4227072 | tf_op jit(solution)/shard_map/stack | solution.py:104
  3.9 11.9 %all-to-all-start = ((bf16[128,16,1024]{2,1,0:T(8,128)(2,1)}), bf16[128,16,1024]{2,1,0:T(8,128)(2,1)}, u32[]{:S(2)}, u32[]{:S(2)}) async-start(bf16[128,16,1024]{2,1,0:T(8,128)(2,1)} %stack.2), calls=%async_computation | async-start | bytes 8388608 | tf_op jit(solution)/shard_map/all_to_all | solution.py:103
  20.3 2.0 %copy.68 = bf16[1,512,512]{1,2,0:T(8,128)(2,1)} copy(bf16[1,512,512]{2,1,0:T(8,128)(2,1)} %param.12) | data formatting | bytes 1048576 | tf_op args[2]
  22.3 2.7 %copy.64 = bf16[1,512,2560]{1,2,0:T(8,128)(2,1)} copy(bf16[1,512,2560]{2,1,0:T(8,128)(2,1)S(1)} %copy-done.5) | data formatting | bytes 5242880 | tf_op args[0]
  25.0 4.4 %copy.69 = bf16[1,512,2560]{1,2,0:T(8,128)(2,1)} copy(bf16[1,512,2560]{2,1,0:T(8,128)(2,1)} %param.15) | data formatting | bytes 5242880 | tf_op args[5]
  30.2 37.6 %all-to-all-done = bf16[128,16,1024]{2,1,0:T(8,128)(2,1)} async-done(((bf16[128,16,1024]{2,1,0:T(8,128)(2,1)}), bf16[128,16,1024]{2,1,0:T(8,128)(2,1)}, u32[]{:S(2)}, u32[]{:S(2)}) %all-to-all-start) | async-done | bytes 4194336 | tf_op jit(solution)/shard_map/all_to_all | solution.py:103
  72.8 1.7 broadcast.75.clone2
  74.5 1.7 broadcast.75.clone
  76.1 95.3 %while.17 = (s32[]{:T(128)}, bf16[512,2560]{1,0:T(8,128)(2,1)}, bf16[512,2560]{1,0:T(8,128)(2,1)}, f32[768,4,128]{0,2,1:T(8,128)}, f32[768,4,128]{0,2,1:T(8,128)...) while((s32[]{:T(128)}, bf16[512,2560]{1,0:T(8,128)(2,1)}, ...), condition=%wide.region_3.4_spmd.clone, body=%wide.region_0.3_spmd.clone.sunk | while | flops 3048635904 | bytes 116517448 | solution.py:82
  76.9 1.5 dynamic-slice_select_fusion.2
  78.4 2.4 %fusion.68 = f32[4,128,5,768]{3,1,2,0:T(8,128)S(1)} fusion(bf16[128,4,5,128]{0,3,2,1:T(8,128)(2,1)S(1)} %bitcast.146, bf16[768,4,128]{0,2,1:T(8,128)(2,1)} %get-tuple-element.289), kind=kOutput, calls=%fused_computation.26.clone.1 | convolution fusion | flops 503316480 | bytes 9306112 | tf_op jit(solution)/shard_map/while/body/tkgd,skd->kgts/dot_general | solution.py:48
  80.7 3.7 %fusion.69 = (f32[4,5,128]{2,1,0:T(8,128)S(1)}, f32[4,5,128,768]{3,2,1,0:T(8,128)S(1)}) fusion(f32[4,128,5,768]{3,1,2,0:T(8,128)S(1)} %fusion.68, pred[128,768]{1,0:T(8,128)(4,1)S(1)} %broadcast_compare_fusion.4), kind=kOutput, calls=%fused_computation.54.clone.1 | output fusion | flops 11797247 | bytes 15837184 | tf_op jit(solution)/shard_map/while/body/sub | solution.py:53
  87.9 3.6 %fusion.72 = bf16[4,5,128,768]{3,2,1,0:T(8,128)(2,1)} fusion(f32[4,5,128]{2,1,0:T(8,128)S(1)} %get-tuple-element.251, f32[4,5,128,768]{3,2,1,0:T(8,128)S(1)} %get-tuple-element.248, f32[4,5,128]{2,1,0:T(8,128)S(1)} %get-tuple-element.249, bf16[128,4,5,128]{0,3,2,1:T(8,128)(2,1)S(1)} %bitcast.150, bf16[768,4,128]{2,0,1:T(8,128)(2,1)S(1)} %copy-done.7), kind=kOutput, calls=%fused_computation.5.clone.1 | convolution fusion | flops 513146880 | bytes 13258752 | tf_op jit(solution)/shard_map/while/body/tkgd,skd->kgts/dot_general | solution.py:58
  91.8 3.7 %convolution_convert_fusion.3 = bf16[4,5,128,128]{2,3,1,0:T(8,128)(2,1)S(1)} fusion(bf16[4,5,128,768]{3,2,1,0:T(8,128)(2,1)} %fusion.72, bf16[768,4,128]{0,2,1:T(8,128)(2,1)} %get-tuple-element.289), kind=kOutput, calls=%fused_computation.19.clone.1 | convolution fusion | flops 503644160 | bytes 5373952 | tf_op jit(solution)/shard_map/while/body/kgts,skd->tkgd/dot_general | solution.py:61
  100.7 1.5 dynamic-slice_select_fusion.2
  102.2 2.4 %fusion.68 = f32[4,128,5,768]{3,1,2,0:T(8,128)S(1)} fusion(bf16[128,4,5,128]{0,3,2,1:T(8,128)(2,1)S(1)} %bitcast.146, bf16[768,4,128]{0,2,1:T(8,128)(2,1)} %get-tuple-element.289), kind=kOutput, calls=%fused_computation.26.clone.1 | convolution fusion | flops 503316480 | bytes 9306112 | tf_op jit(solution)/shard_map/while/body/tkgd,skd->kgts/dot_general | solution.py:48
  104.6 3.7 %fusion.69 = (f32[4,5,128]{2,1,0:T(8,128)S(1)}, f32[4,5,128,768]{3,2,1,0:T(8,128)S(1)}) fusion(f32[4,128,5,768]{3,1,2,0:T(8,128)S(1)} %fusion.68, pred[128,768]{1,0:T(8,128)(4,1)S(1)} %broadcast_compare_fusion.4), kind=kOutput, calls=%fused_computation.54.clone.1 | output fusion | flops 11797247 | bytes 15837184 | tf_op jit(solution)/shard_map/while/body/sub | solution.py:53
  111.7 3.6 %fusion.72 = bf16[4,5,128,768]{3,2,1,0:T(8,128)(2,1)} fusion(f32[4,5,128]{2,1,0:T(8,128)S(1)} %get-tuple-element.251, f32[4,5,128,768]{3,2,1,0:T(8,128)S(1)} %get-tuple-element.248, f32[4,5,128]{2,1,0:T(8,128)S(1)} %get-tuple-element.249, bf16[128,4,5,128]{0,3,2,1:T(8,128)(2,1)S(1)} %bitcast.150, bf16[768,4,128]{2,0,1:T(8,128)(2,1)S(1)} %copy-done.7), kind=kOutput, calls=%fused_computation.5.clone.1 | convolution fusion | flops 513146880 | bytes 13258752 | tf_op jit(solution)/shard_map/while/body/tkgd,skd->kgts/dot_general | solution.py:58
  115.6 3.7 %convolution_convert_fusion.3 = bf16[4,5,128,128]{2,3,1,0:T(8,128)(2,1)S(1)} fusion(bf16[4,5,128,768]{3,2,1,0:T(8,128)(2,1)} %fusion.72, bf16[768,4,128]{0,2,1:T(8,128)(2,1)} %get-tuple-element.289), kind=kOutput, calls=%fused_computation.19.clone.1 | convolution fusion | flops 503644160 | bytes 5373952 | tf_op jit(solution)/shard_map/while/body/kgts,skd->tkgd/dot_general | solution.py:61
  124.6 1.5 dynamic-slice_select_fusion.2
  126.0 2.4 %fusion.68 = f32[4,128,5,768]{3,1,2,0:T(8,128)S(1)} fusion(bf16[128,4,5,128]{0,3,2,1:T(8,128)(2,1)S(1)} %bitcast.146, bf16[768,4,128]{0,2,1:T(8,128)(2,1)} %get-tuple-element.289), kind=kOutput, calls=%fused_computation.26.clone.1 | convolution fusion | flops 503316480 | bytes 9306112 | tf_op jit(solution)/shard_map/while/body/tkgd,skd->kgts/dot_general | solution.py:48
  128.4 3.7 %fusion.69 = (f32[4,5,128]{2,1,0:T(8,128)S(1)}, f32[4,5,128,768]{3,2,1,0:T(8,128)S(1)}) fusion(f32[4,128,5,768]{3,1,2,0:T(8,128)S(1)} %fusion.68, pred[128,768]{1,0:T(8,128)(4,1)S(1)} %broadcast_compare_fusion.4), kind=kOutput, calls=%fused_computation.54.clone.1 | output fusion | flops 11797247 | bytes 15837184 | tf_op jit(solution)/shard_map/while/body/sub | solution.py:53
  135.5 3.6 %fusion.72 = bf16[4,5,128,768]{3,2,1,0:T(8,128)(2,1)} fusion(f32[4,5,128]{2,1,0:T(8,128)S(1)} %get-tuple-element.251, f32[4,5,128,768]{3,2,1,0:T(8,128)S(1)} %get-tuple-element.248, f32[4,5,128]{2,1,0:T(8,128)S(1)} %get-tuple-element.249, bf16[128,4,5,128]{0,3,2,1:T(8,128)(2,1)S(1)} %bitcast.150, bf16[768,4,128]{2,0,1:T(8,128)(2,1)S(1)} %copy-done.7), kind=kOutput, calls=%fused_computation.5.clone.1 | convolution fusion | flops 513146880 | bytes 13258752 | tf_op jit(solution)/shard_map/while/body/tkgd,skd->kgts/dot_general | solution.py:58
  139.4 3.7 %convolution_convert_fusion.3 = bf16[4,5,128,128]{2,3,1,0:T(8,128)(2,1)S(1)} fusion(bf16[4,5,128,768]{3,2,1,0:T(8,128)(2,1)} %fusion.72, bf16[768,4,128]{0,2,1:T(8,128)(2,1)} %get-tuple-element.289), kind=kOutput, calls=%fused_computation.19.clone.1 | convolution fusion | flops 503644160 | bytes 5373952 | tf_op jit(solution)/shard_map/while/body/kgts,skd->tkgd/dot_general | solution.py:61
  149.8 2.4 %fusion.68 = f32[4,128,5,768]{3,1,2,0:T(8,128)S(1)} fusion(bf16[128,4,5,128]{0,3,2,1:T(8,128)(2,1)S(1)} %bitcast.146, bf16[768,4,128]{0,2,1:T(8,128)(2,1)} %get-tuple-element.289), kind=kOutput, calls=%fused_computation.26.clone.1 | convolution fusion | flops 503316480 | bytes 9306112 | tf_op jit(solution)/shard_map/while/body/tkgd,skd->kgts/dot_general | solution.py:48
  152.2 3.7 %fusion.69 = (f32[4,5,128]{2,1,0:T(8,128)S(1)}, f32[4,5,128,768]{3,2,1,0:T(8,128)S(1)}) fusion(f32[4,128,5,768]{3,1,2,0:T(8,128)S(1)} %fusion.68, pred[128,768]{1,0:T(8,128)(4,1)S(1)} %broadcast_compare_fusion.4), kind=kOutput, calls=%fused_computation.54.clone.1 | output fusion | flops 11797247 | bytes 15837184 | tf_op jit(solution)/shard_map/while/body/sub | solution.py:53
  159.3 3.6 %fusion.72 = bf16[4,5,128,768]{3,2,1,0:T(8,128)(2,1)} fusion(f32[4,5,128]{2,1,0:T(8,128)S(1)} %get-tuple-element.251, f32[4,5,128,768]{3,2,1,0:T(8,128)S(1)} %get-tuple-element.248, f32[4,5,128]{2,1,0:T(8,128)S(1)} %get-tuple-element.249, bf16[128,4,5,128]{0,3,2,1:T(8,128)(2,1)S(1)} %bitcast.150, bf16[768,4,128]{2,0,1:T(8,128)(2,1)S(1)} %copy-done.7), kind=kOutput, calls=%fused_computation.5.clone.1 | convolution fusion | flops 513146880 | bytes 13258752 | tf_op jit(solution)/shard_map/while/body/tkgd,skd->kgts/dot_general | solution.py:58
  163.2 3.7 %convolution_convert_fusion.3 = bf16[4,5,128,128]{2,3,1,0:T(8,128)(2,1)S(1)} fusion(bf16[4,5,128,768]{3,2,1,0:T(8,128)(2,1)} %fusion.72, bf16[768,4,128]{0,2,1:T(8,128)(2,1)} %get-tuple-element.289), kind=kOutput, calls=%fused_computation.19.clone.1 | convolution fusion | flops 503644160 | bytes 5373952 | tf_op jit(solution)/shard_map/while/body/kgts,skd->tkgd/dot_general | solution.py:61
  174.4 4.4 %all-to-all-start.1 = ((bf16[1,16,16,1024]{3,2,0,1:T(8,128)(2,1)}), bf16[1,16,16,1024]{3,2,0,1:T(8,128)(2,1)S(1)}, u32[]{:S(2)}, u32[]{:S(2)}) async-start(bf16[1,16,16,1024]{3,2,0,1:T(8,128)(2,1)} %maximum_bitcast_fusion), calls=%async_computation.1 | async-start | bytes 1048576 | tf_op jit(solution)/shard_map/all_to_all | solution.py:123
  178.9 10.1 %all-to-all-done.1 = bf16[1,16,16,1024]{3,2,0,1:T(8,128)(2,1)S(1)} async-done(((bf16[1,16,16,1024]{3,2,0,1:T(8,128)(2,1)}), bf16[1,16,16,1024]{3,2,0,1:T(8,128)(2,1)S(1)}, u32[]{:S(2)}, u32[]{:S(2)}) %all-to-all-start.1) | async-done | bytes 524320 | tf_op jit(solution)/shard_map/all_to_all | solution.py:123
  190.2 5.6 %all-to-all-start.2 = ((bf16[8,1,16,1024]{3,2,1,0:T(8,128)(2,1)}), bf16[8,1,16,1024]{3,2,1,0:T(8,128)(2,1)S(1)}, u32[]{:S(2)}, u32[]{:S(2)}) async-start(bf16[8,1,16,1024]{3,2,1,0:T(8,128)(2,1)} %copy.79), calls=%async_computation.2 | async-start | bytes 524288 | tf_op jit(solution)/shard_map/all_to_all | solution.py:19
  197.9 4.4 %all-to-all-done.2 = bf16[8,1,16,1024]{3,2,1,0:T(8,128)(2,1)S(1)} async-done(((bf16[8,1,16,1024]{3,2,1,0:T(8,128)(2,1)}), bf16[8,1,16,1024]{3,2,1,0:T(8,128)(2,1)S(1)}, u32[]{:S(2)}, u32[]{:S(2)}) %all-to-all-start.2) | async-done | bytes 262176 | tf_op jit(solution)/shard_map/all_to_all | solution.py:19
  (127 shorter events, 52.0 us)
Async XLA Ops:
  3.9 12.0 %copy-start.8 = (s32[128]{0:T(128)S(1)}, s32[128]{0:T(128)}, u32[]{:S(2)}) copy-start(s32[128]{0:T(128)} %param.16) | copy-start | bytes 1540
  3.9 13.2 %copy-start.9 = (s32[128]{0:T(128)S(1)}, s32[128]{0:T(128)}, u32[]{:S(2)}) copy-start(s32[128]{0:T(128)} %param.17) | copy-start | bytes 1540
  3.9 18.4 %copy-start.5 = (bf16[1,512,2560]{2,1,0:T(8,128)(2,1)S(1)}, bf16[1,512,2560]{2,1,0:T(8,128)(2,1)}, u32[]{:S(2)}) copy-start(bf16[1,512,2560]{2,1,0:T(8,128)(2,1)} %param.10) | copy-start | bytes 7864324
  3.9 63.9 %all-to-all-start = ((bf16[128,16,1024]{2,1,0:T(8,128)(2,1)}), bf16[128,16,1024]{2,1,0:T(8,128)(2,1)}, u32[]{:S(2)}, u32[]{:S(2)}) async-start(bf16[128,16,1024]{2,1,0:T(8,128)(2,1)} %stack.2), calls=%async_computation | async-start | bytes 8388608 | tf_op jit(solution)/shard_map/all_to_all | solution.py:103
  29.4 39.6 %copy-start.6 = (bf16[1,512,512]{1,2,0:T(8,128)(2,1)S(1)}, bf16[1,512,512]{1,2,0:T(8,128)(2,1)}, u32[]{:S(2)}) copy-start(bf16[1,512,512]{1,2,0:T(8,128)(2,1)} %copy.68) | copy-start | bytes 1572868
  84.4 1.1 copy-start.7
  91.8 3.8 %copy-start = (bf16[4,5,128,768]{3,2,1,0:T(8,128)(2,1)S(1)}, bf16[4,5,128,768]{3,2,1,0:T(8,128)(2,1)}, u32[]{:S(2)}) copy-start(bf16[4,5,128,768]{3,2,1,0:T(8,128)(2,1)} %fusion.72) | copy-start | bytes 11796484 | tf_op jit(solution)/shard_map/while
  91.8 4.0 %copy-start.1 = (f32[768,4,128]{0,2,1:T(8,128)S(1)}, f32[768,4,128]{0,2,1:T(8,128)}, u32[]{:S(2)}) copy-start(f32[768,4,128]{0,2,1:T(8,128)} %get-tuple-element.270) | copy-start | bytes 4718596 | tf_op jit(solution)/shard_map/while
  96.8 1.2 copy-start.2
  108.2 1.1 copy-start.7
  115.6 3.8 %copy-start = (bf16[4,5,128,768]{3,2,1,0:T(8,128)(2,1)S(1)}, bf16[4,5,128,768]{3,2,1,0:T(8,128)(2,1)}, u32[]{:S(2)}) copy-start(bf16[4,5,128,768]{3,2,1,0:T(8,128)(2,1)} %fusion.72) | copy-start | bytes 11796484 | tf_op jit(solution)/shard_map/while
  115.6 4.0 %copy-start.1 = (f32[768,4,128]{0,2,1:T(8,128)S(1)}, f32[768,4,128]{0,2,1:T(8,128)}, u32[]{:S(2)}) copy-start(f32[768,4,128]{0,2,1:T(8,128)} %get-tuple-element.270) | copy-start | bytes 4718596 | tf_op jit(solution)/shard_map/while
  120.6 1.2 copy-start.2
  132.1 1.1 copy-start.7
  139.4 3.8 %copy-start = (bf16[4,5,128,768]{3,2,1,0:T(8,128)(2,1)S(1)}, bf16[4,5,128,768]{3,2,1,0:T(8,128)(2,1)}, u32[]{:S(2)}) copy-start(bf16[4,5,128,768]{3,2,1,0:T(8,128)(2,1)} %fusion.72) | copy-start | bytes 11796484 | tf_op jit(solution)/shard_map/while
  139.4 4.0 %copy-start.1 = (f32[768,4,128]{0,2,1:T(8,128)S(1)}, f32[768,4,128]{0,2,1:T(8,128)}, u32[]{:S(2)}) copy-start(f32[768,4,128]{0,2,1:T(8,128)} %get-tuple-element.270) | copy-start | bytes 4718596 | tf_op jit(solution)/shard_map/while
  144.4 1.2 copy-start.2
  155.9 1.1 copy-start.7
  163.2 3.8 %copy-start = (bf16[4,5,128,768]{3,2,1,0:T(8,128)(2,1)S(1)}, bf16[4,5,128,768]{3,2,1,0:T(8,128)(2,1)}, u32[]{:S(2)}) copy-start(bf16[4,5,128,768]{3,2,1,0:T(8,128)(2,1)} %fusion.72) | copy-start | bytes 11796484 | tf_op jit(solution)/shard_map/while
  163.2 4.0 %copy-start.1 = (f32[768,4,128]{0,2,1:T(8,128)S(1)}, f32[768,4,128]{0,2,1:T(8,128)}, u32[]{:S(2)}) copy-start(f32[768,4,128]{0,2,1:T(8,128)} %get-tuple-element.270) | copy-start | bytes 4718596 | tf_op jit(solution)/shard_map/while
  168.2 1.2 copy-start.2
  171.4 1.7 copy-start.3
  171.5 0.9 copy-start.4
  173.1 5.7 %copy-start.10 = (s32[128]{0:T(128)S(1)}, s32[128]{0:T(128)}, u32[]{:S(2)}) copy-start(s32[128]{0:T(128)} %param.17) | copy-start | bytes 1540
  174.4 21.5 %slice-start = ((bf16[768,4,128]{0,2,1:T(8,128)(2,1)}), bf16[512,4,128]{0,2,1:T(8,128)(2,1)S(1)}, s32[]{:S(2)}) async-start(bf16[768,4,128]{0,2,1:T(8,128)(2,1)} %copy-done.4), calls=%async_computation.3 | async-start | bytes 1048576 | tf_op jit(solution)/shard_map/slice | solution.py:119
  174.4 14.6 %all-to-all-start.1 = ((bf16[1,16,16,1024]{3,2,0,1:T(8,128)(2,1)}), bf16[1,16,16,1024]{3,2,0,1:T(8,128)(2,1)S(1)}, u32[]{:S(2)}, u32[]{:S(2)}) async-start(bf16[1,16,16,1024]{3,2,0,1:T(8,128)(2,1)} %maximum_bitcast_fusion), calls=%async_computation.1 | async-start | bytes 1048576 | tf_op jit(solution)/shard_map/all_to_all | solution.py:123
  190.2 12.1 %all-to-all-start.2 = ((bf16[8,1,16,1024]{3,2,1,0:T(8,128)(2,1)}), bf16[8,1,16,1024]{3,2,1,0:T(8,128)(2,1)S(1)}, u32[]{:S(2)}, u32[]{:S(2)}) async-start(bf16[8,1,16,1024]{3,2,1,0:T(8,128)(2,1)} %copy.79), calls=%async_computation.2 | async-start | bytes 524288 | tf_op jit(solution)/shard_map/all_to_all | solution.py:19
